TPU v7x, 256 devices: a whole 4x4x8 slice. The times are simulated.
256 devices in a mesh: row: 16 (over x_hi, z), col: 16 (over x_lo, y, core).
Axes of the slice: x: 4 (x_hi: 2, x_lo: 2; x = x_hi * 2 + x_lo), y: 4, z: 8, core: 2. Of those that a mesh axis runs over, the one named last changes fastest.
Arguments:
- southeast_edges: bfloat16 [16, 16, 2, 2, 2, 96, 768], P('row', 'col'), may hold values from -6 to 6
- northwest_edges: bfloat16 [16, 16, 2, 2, 2, 96, 768], P('row', 'col'), may hold values from -6 to 6
- southeast_corners: bfloat16 [16, 16, 2, 2, 96, 128], P('row', 'col'), may hold values from -6 to 6
- northwest_corners: bfloat16 [16, 16, 2, 2, 96, 128], P('row', 'col'), may hold values from -6 to 6
- operators: bfloat16 [16, 16, 2, 2, 768, 768], P('row', 'col'), may hold values from -0.109375 to 0.109375
- sources: bfloat16 [16, 16, 2, 2, 96, 768], P('row', 'col'), may hold values from -3 to 3
- roster: int32 [2, 3, 2], replicated, may hold values from 0 to 1, as said below
Outputs:
- southeast_out: bfloat16 [16, 16, 2, 2, 2, 96, 768], P('row', 'col')
- northwest_out: bfloat16 [16, 16, 2, 2, 2, 96, 768], P('row', 'col')
- southeast_corner_out: bfloat16 [16, 16, 2, 2, 96, 128], P('row', 'col')
- northwest_corner_out: bfloat16 [16, 16, 2, 2, 96, 128], P('row', 'col')
Inputs may be any that keep to these rules, and one draw needn't show every extreme that they name: roster[d, k, b] is the class, modulo 2, of the antidiagonals on which batch b of direction d stands at tick k. It rises by one modulo 2 from each tick to the next, and at every tick the 2 batches of one direction take all classes, each once.
All inputs are finite; a program needn't handle non-finite values.
Results may differ from a plain program's by a relative error of at most 0.0051.
Values may be sent and summed in bfloat16 or wider, within the bound.
A program may use at most 64 MiB of HBM per device.

v0:
```python
import jax
import jax.numpy as jnp
from jax import lax
from jax.sharding import PartitionSpec as P

TICKS = 3


def from_behind(array, axis, by):
    count = lax.axis_size(axis)
    return lax.ppermute(array, axis, [(i, (i + by) % count) for i in range(count)])


def trace_update(first_in, second_in, corner_in, cell_operators, source, flipped):
    shot_count = first_in.shape[1]
    edge_width = first_in.shape[2]
    corner_width = corner_in.shape[-1]
    stacked = jnp.stack([first_in, second_in]).reshape(4 * shot_count, edge_width)
    form = "qe,mpfe->mpqf" if flipped else "qe,mpef->mpqf"
    products = jnp.einsum(form, stacked, cell_operators, preferred_element_type=jnp.float32)
    products = products.reshape(2, 2, 2, 2, shot_count, edge_width)

    def complex_product(source_index, operator_index):
        real_part = (
            products[operator_index, 0, source_index, 0]
            - products[operator_index, 1, source_index, 1]
        )
        imag_part = (
            products[operator_index, 1, source_index, 0]
            + products[operator_index, 0, source_index, 1]
        )
        return jnp.stack([real_part, imag_part])

    source_value = source.astype(jnp.float32)
    corner_value = corner_in.astype(jnp.float32)
    first_out = complex_product(0, 0) + complex_product(1, 1) + source_value
    second_out = complex_product(0, 1) + complex_product(1, 0) + source_value
    if flipped:
        first_out = first_out.at[:, :, edge_width - corner_width :].add(corner_value)
        second_out = second_out.at[:, :, edge_width - corner_width :].add(corner_value)
        corner_out = 0.5 * (first_out[:, :, :corner_width] + second_out[:, :, :corner_width])
    else:
        first_out = first_out.at[:, :, :corner_width].add(corner_value)
        second_out = second_out.at[:, :, :corner_width].add(corner_value)
        corner_out = 0.5 * (
            first_out[:, :, edge_width - corner_width :]
            + second_out[:, :, edge_width - corner_width :]
        )
    return (
        first_out.astype(jnp.bfloat16),
        second_out.astype(jnp.bfloat16),
        corner_out.astype(jnp.bfloat16),
    )


def southeast_moves(first_send, second_send, corner_send):
    from_north = from_behind(first_send, "row", 1)
    from_west = from_behind(second_send, "col", 1)
    corner_half = from_behind(corner_send, "row", 1)
    from_corner = from_behind(corner_half, "col", 1)
    return (from_north, from_west, from_corner)


def northwest_moves(first_send, second_send, corner_send):
    from_south = from_behind(first_send, "row", -1)
    from_east = from_behind(second_send, "col", -1)
    corner_half = from_behind(corner_send, "row", -1)
    from_corner = from_behind(corner_half, "col", -1)
    return (from_south, from_east, from_corner)


def sweep_tick(
    states, corner_states, front_plan, frame_row, frame_col, local_operators, local_sources, flipped
):
    batch_count = front_plan.shape[0]
    klass = (frame_row + frame_col) % batch_count
    first_send = states[0]
    second_send = states[1]
    corner_send = corner_states
    if flipped:
        got_first, got_second, got_corner = northwest_moves(first_send, second_send, corner_send)
    else:
        got_first, got_second, got_corner = southeast_moves(first_send, second_send, corner_send)
    chosen = jnp.argmax((front_plan == klass).astype(jnp.int32))
    first_in = got_first[chosen]
    second_in = got_second[chosen]
    corner_in = got_corner[chosen]
    new_first, new_second, new_corner = trace_update(
        first_in, second_in, corner_in, local_operators, local_sources[chosen], flipped
    )
    states = states.at[:, chosen].set(jnp.stack([new_first, new_second]))
    corner_states = corner_states.at[chosen].set(new_corner)
    return (states, corner_states)


def shards(
    southeast_edges,
    northwest_edges,
    southeast_corners,
    northwest_corners,
    operators,
    sources,
    roster,
):
    down_states = southeast_edges[0, 0]
    up_states = northwest_edges[0, 0]
    down_corners = southeast_corners[0, 0]
    up_corners = northwest_corners[0, 0]
    local_operators = operators[0, 0]
    local_sources = sources[0, 0]
    row_count = lax.axis_size("row")
    col_count = lax.axis_size("col")
    row_place = lax.axis_index("row")
    col_place = lax.axis_index("col")
    up_row = row_count - 1 - row_place
    up_col = col_count - 1 - col_place
    for tick_index in range(TICKS):
        down_states, down_corners = sweep_tick(
            down_states,
            down_corners,
            roster[0, tick_index],
            row_place,
            col_place,
            local_operators,
            local_sources,
            False,
        )
        up_states, up_corners = sweep_tick(
            up_states,
            up_corners,
            roster[1, tick_index],
            up_row,
            up_col,
            local_operators,
            local_sources,
            True,
        )
    return (
        down_states[None, None],
        up_states[None, None],
        down_corners[None, None],
        up_corners[None, None],
    )


def solution(mesh):
    placed = (
        P("row", "col", None, None, None, None, None),
        P("row", "col", None, None, None, None, None),
        P("row", "col", None, None, None, None),
        P("row", "col", None, None, None, None),
        P("row", "col", None, None, None, None),
        P("row", "col", None, None, None, None),
        P(),
    )
    return jax.shard_map(
        shards,
        mesh=mesh,
        in_specs=placed,
        out_specs=(
            P("row", "col", None, None, None, None, None),
            P("row", "col", None, None, None, None, None),
            P("row", "col", None, None, None, None),
            P("row", "col", None, None, None, None),
        ),
        check_vma=False,
    )
```

profile of v0, /device:TPU:4, one launch (start us, length us, event | category | flops | bytes accessed | tf_op | source)
XLA Modules:
  0.0 166.7 jit_solution(9088099296294012235)
XLA Ops:
  0.6 2.4 %slice_bitcast_fusion.9 = (bf16[2,2,96,768]{3,2,1,0:T(8,128)(2,1)}, bf16[2,2,96,768]{3,2,1,0:T(8,128)(2,1)}) fusion(bf16[1,1,2,2,2,96,768]{6,5,4,3,2,1,0:T(8,128)(2,1)} %param.56), kind=kLoop, calls=%fused_computation.71 | loop fusion | bytes 2359296 | tf_op jit(solution)/shard_map/squeeze | solution.py:77
  3.1 3.1 %collective-permute-start.13 = (bf16[2,2,96,768]{3,2,1,0:T(8,128)(2,1)}, bf16[2,2,96,768]{3,2,1,0:T(8,128)(2,1)}, u32[]{:S(2)}, u32[]{:S(2)}) collective-permute-start(bf16[2,2,96,768]{3,2,1,0:T(8,128)(2,1)} %get-tuple-element.379), channel_id=1, source_target_pairs={{0,15},{1,0},{2,1},{3,2},{4,3},{5,4},{6,5},{7,6},{8,7},{9,8},{10,9... | collective-permute-start | bytes 1769480 | tf_op jit(solution)/shard_map/ppermute | solution.py:11
  6.2 6.1 %collective-permute-start.12 = (bf16[2,2,96,768]{3,2,1,0:T(8,128)(2,1)}, bf16[2,2,96,768]{3,2,1,0:T(8,128)(2,1)}, u32[]{:S(2)}, u32[]{:S(2)}) collective-permute-start(bf16[2,2,96,768]{3,2,1,0:T(8,128)(2,1)} %get-tuple-element.378), channel_id=1, source_target_pairs={{0,240},{16,0},{32,16},{48,32},{64,48},{80,64},{96,80},{112,96},{1... | collective-permute-start | bytes 1769480 | tf_op jit(solution)/shard_map/ppermute | solution.py:11
  13.3 1.1 slice_bitcast_fusion.11
  14.3 1.0 collective-permute-start.2
  22.2 1.5 copy.38
  28.6 1.6 copy.45
  37.7 1.5 and_reduce_fusion.3
  39.9 3.6 %collective-permute-start.15 = (bf16[2,2,96,128]{3,2,1,0:T(8,128)(2,1)}, bf16[2,2,96,128]{3,2,1,0:T(8,128)(2,1)S(1)}, u32[]{:S(2)}, u32[]{:S(2)}) collective-permute-start(bf16[2,2,96,128]{3,2,1,0:T(8,128)(2,1)} %collective-permute-done.14), channel_id=1, source_target_pairs={{0,15},{1,0},{2,1},{3,2},{4,3},{5,4},{6,5},{7,6},{8,7},{9,8},{10,9... | collective-permute-start | bytes 294920 | tf_op jit(solution)/shard_map/ppermute | solution.py:11
  45.6 4.5 %fusion.4 = f32[384,2,2,768]{3,0,2,1:T(8,128)S(1)} fusion(bf16[384,768,1,1]{1,0,3,2:T(8,128)(2,1)S(1)} %bitcast.390, bf16[1,1,2,2,768,768]{5,4,3,2,1,0:T(8,128)(2,1)} %param.59), kind=kOutput, calls=%fused_computation.4 | convolution fusion | flops 1811939328 | bytes 10027008 | tf_op jit(solution)/shard_map/qe,mpfe->mpqf/dot_general | solution.py:20
  51.4 5.8 %collective-permute-done.15 = bf16[2,2,96,128]{3,2,1,0:T(8,128)(2,1)S(1)} collective-permute-done((bf16[2,2,96,128]{3,2,1,0:T(8,128)(2,1)}, bf16[2,2,96,128]{3,2,1,0:T(8,128)(2,1)S(1)}, u32[]{:S(2)}, u32[]{:S(2)}) %collective-permute-start.15) | collective-permute-done | bytes 98336 | tf_op jit(solution)/shard_map/ppermute | solution.py:11
  58.3 4.0 %collective-permute-start.17 = (bf16[2,2,96,768]{3,2,1,0:T(8,128)(2,1)S(1)}, bf16[2,2,96,768]{3,2,1,0:T(8,128)(2,1)S(1)}, u32[]{:S(2)}, u32[]{:S(2)}) collective-permute-start(bf16[2,2,96,768]{3,2,1,0:T(8,128)(2,1)S(1)} %get-tuple-element.377), channel_id=1, source_target_pairs={{0,15},{1,0},{2,1},{3,2},{4,3},{5,4},{6,5},{7,6},{8,7},{9,8},{10,9... | collective-permute-start | bytes 1769480 | tf_op jit(solution)/shard_map/ppermute | solution.py:11
  62.3 1.5 fusion.104
  65.1 5.1 %collective-permute-done.18 = bf16[2,2,96,128]{3,2,1,0:T(8,128)(2,1)S(1)} collective-permute-done((bf16[2,2,96,128]{3,2,1,0:T(8,128)(2,1)S(1)}, bf16[2,2,96,128]{3,2,1,0:T(8,128)(2,1)S(1)}, u32[]{:S(2)}, u32[]{:S(2)}) %collective-permute-start.18) | collective-permute-done | bytes 98336 | tf_op jit(solution)/shard_map/ppermute | solution.py:11
  70.3 3.6 %collective-permute-start.19 = (bf16[2,2,96,128]{3,2,1,0:T(8,128)(2,1)S(1)}, bf16[2,2,96,128]{3,2,1,0:T(8,128)(2,1)S(1)}, u32[]{:S(2)}, u32[]{:S(2)}) collective-permute-start(bf16[2,2,96,128]{3,2,1,0:T(8,128)(2,1)S(1)} %collective-permute-done.18), channel_id=1, source_target_pairs={{0,15},{1,0},{2,1},{3,2},{4,3},{5,4},{6,5},{7,6},{8,7},{9,8},{10,9... | collective-permute-start | bytes 294920 | tf_op jit(solution)/shard_map/ppermute | solution.py:11
  74.0 2.0 %fusion.2 = f32[384,2,2,768]{3,0,2,1:T(8,128)S(1)} fusion(bf16[384,768,1,1]{1,0,3,2:T(8,128)(2,1)S(1)} %bitcast.391, bf16[1,1,2,2,768,768]{5,4,3,2,1,0:T(8,128)(2,1)S(1)} %bitcast.396), kind=kOutput, calls=%fused_computation.2 | convolution fusion | flops 1811939328 | bytes 10027008 | tf_op jit(solution)/shard_map/qe,mpfe->mpqf/dot_general | solution.py:20
  77.6 7.2 %collective-permute-start.20 = (bf16[2,2,96,768]{3,2,1,0:T(8,128)(2,1)S(1)}, bf16[2,2,96,768]{3,2,1,0:T(8,128)(2,1)S(1)}, u32[]{:S(2)}, u32[]{:S(2)}) collective-permute-start(bf16[2,2,96,768]{3,2,1,0:T(8,128)(2,1)S(1)} %get-tuple-element.374), channel_id=1, source_target_pairs={{0,240},{16,0},{32,16},{48,32},{64,48},{80,64},{96,80},{112,96},{1... | collective-permute-start | bytes 1769480 | tf_op jit(solution)/shard_map/ppermute | solution.py:11
  84.9 2.0 %fusion.10 = f32[384,2,2,768]{3,0,2,1:T(8,128)S(1)} fusion(bf16[384,768,1,1]{1,0,3,2:T(8,128)(2,1)S(1)} %bitcast.389, bf16[1,1,2,2,768,768]{5,4,3,2,1,0:T(8,128)(2,1)S(1)} %bitcast.396), kind=kOutput, calls=%fused_computation.10 | convolution fusion | flops 1811939328 | bytes 10027008 | tf_op jit(solution)/shard_map/qe,mpef->mpqf/dot_general | solution.py:20
  86.9 4.4 %collective-permute-start.21 = (bf16[2,2,96,768]{3,2,1,0:T(8,128)(2,1)S(1)}, bf16[2,2,96,768]{3,2,1,0:T(8,128)(2,1)S(1)}, u32[]{:S(2)}, u32[]{:S(2)}) collective-permute-start(bf16[2,2,96,768]{3,2,1,0:T(8,128)(2,1)S(1)} %get-tuple-element.375), channel_id=1, source_target_pairs={{0,15},{1,0},{2,1},{3,2},{4,3},{5,4},{6,5},{7,6},{8,7},{9,8},{10,9... | collective-permute-start | bytes 1769480 | tf_op jit(solution)/shard_map/ppermute | solution.py:11
  92.5 4.2 %collective-permute-done.22 = bf16[2,2,96,128]{3,2,1,0:T(8,128)(2,1)S(1)} collective-permute-done((bf16[2,2,96,128]{3,2,1,0:T(8,128)(2,1)S(1)}, bf16[2,2,96,128]{3,2,1,0:T(8,128)(2,1)S(1)}, u32[]{:S(2)}, u32[]{:S(2)}) %collective-permute-start.22) | collective-permute-done | bytes 98336 | tf_op jit(solution)/shard_map/ppermute | solution.py:11
  96.6 1.7 %collective-permute-start.23 = (bf16[2,2,96,128]{3,2,1,0:T(8,128)(2,1)S(1)}, bf16[2,2,96,128]{3,2,1,0:T(8,128)(2,1)S(1)}, u32[]{:S(2)}, u32[]{:S(2)}) collective-permute-start(bf16[2,2,96,128]{3,2,1,0:T(8,128)(2,1)S(1)} %collective-permute-done.22), channel_id=1, source_target_pairs={{0,15},{1,0},{2,1},{3,2},{4,3},{5,4},{6,5},{7,6},{8,7},{9,8},{10,9... | collective-permute-start | bytes 294920 | tf_op jit(solution)/shard_map/ppermute | solution.py:11
  98.8 2.0 %fusion = f32[384,2,2,768]{3,0,2,1:T(8,128)S(1)} fusion(bf16[384,768,1,1]{1,0,3,2:T(8,128)(2,1)S(1)} %bitcast.392, bf16[1,1,2,2,768,768]{5,4,3,2,1,0:T(8,128)(2,1)S(1)} %bitcast.396), kind=kOutput, calls=%fused_computation | convolution fusion | flops 1811939328 | bytes 10027008 | tf_op jit(solution)/shard_map/qe,mpfe->mpqf/dot_general | solution.py:20
  101.8 1.1 copy-done.3
  104.6 1.4 fusion.98
  106.5 16.9 %collective-permute-done.6 = bf16[2,2,96,128]{3,2,1,0:T(8,128)(2,1)S(1)} collective-permute-done((bf16[2,2,96,128]{3,2,1,0:T(8,128)(2,1)S(1)}, bf16[2,2,96,128]{3,2,1,0:T(8,128)(2,1)S(1)}, u32[]{:S(2)}, u32[]{:S(2)}) %collective-permute-start.6) | collective-permute-done | bytes 98336 | tf_op jit(solution)/shard_map/ppermute | solution.py:11
  123.4 7.8 %collective-permute-done.5 = bf16[2,2,96,768]{3,2,1,0:T(8,128)(2,1)S(1)} collective-permute-done((bf16[2,2,96,768]{3,2,1,0:T(8,128)(2,1)S(1)}, bf16[2,2,96,768]{3,2,1,0:T(8,128)(2,1)S(1)}, u32[]{:S(2)}, u32[]{:S(2)}) %collective-permute-start.5) | collective-permute-done | bytes 589856 | tf_op jit(solution)/shard_map/ppermute | solution.py:11
  131.3 2.0 %fusion.8 = f32[384,2,2,768]{3,0,2,1:T(8,128)S(1)} fusion(bf16[384,768,1,1]{1,0,3,2:T(8,128)(2,1)S(1)} %bitcast.393, bf16[1,1,2,2,768,768]{5,4,3,2,1,0:T(8,128)(2,1)S(1)} %bitcast.396), kind=kOutput, calls=%fused_computation.8 | convolution fusion | flops 1811939328 | bytes 10027008 | tf_op jit(solution)/shard_map/qe,mpef->mpqf/dot_general | solution.py:20
  137.2 1.1 copy.20
  138.4 11.1 %collective-permute-done.10 = bf16[2,2,96,128]{3,2,1,0:T(8,128)(2,1)S(1)} collective-permute-done((bf16[2,2,96,128]{3,2,1,0:T(8,128)(2,1)S(1)}, bf16[2,2,96,128]{3,2,1,0:T(8,128)(2,1)S(1)}, u32[]{:S(2)}, u32[]{:S(2)}) %collective-permute-start.10) | collective-permute-done | bytes 98336 | tf_op jit(solution)/shard_map/ppermute | solution.py:11
  149.6 11.2 %collective-permute-done.9 = bf16[2,2,96,768]{3,2,1,0:T(8,128)(2,1)S(1)} collective-permute-done((bf16[2,2,96,768]{3,2,1,0:T(8,128)(2,1)S(1)}, bf16[2,2,96,768]{3,2,1,0:T(8,128)(2,1)S(1)}, u32[]{:S(2)}, u32[]{:S(2)}) %collective-permute-start.9) | collective-permute-done | bytes 589856 | tf_op jit(solution)/shard_map/ppermute | solution.py:11
  160.9 2.0 %fusion.6 = f32[384,2,2,768]{3,0,2,1:T(8,128)S(1)} fusion(bf16[384,768,1,1]{1,0,3,2:T(8,128)(2,1)S(1)} %bitcast.394, bf16[1,1,2,2,768,768]{5,4,3,2,1,0:T(8,128)(2,1)S(1)} %bitcast.396), kind=kOutput, calls=%fused_computation.6 | convolution fusion | flops 1811939328 | bytes 10027008 | tf_op jit(solution)/shard_map/qe,mpef->mpqf/dot_general | solution.py:20
  164.4 1.1 copy.19
  (140 shorter events, 28.6 us)
Async XLA Ops:
  0.6 12.6 %copy-start.1 = (bf16[1,1,2,2,2,96,768]{6,5,4,3,2,1,0:T(8,128)(2,1)S(1)}, bf16[1,1,2,2,2,96,768]{6,5,4,3,2,1,0:T(8,128)(2,1)}, u32[]{:S(2)}) copy-start(bf16[1,1,2,2,2,96,768]{6,5,4,3,2,1,0:T(8,128)(2,1)} %param.55) | copy-start | bytes 3538948
  3.1 40.5 %collective-permute-start.13 = (bf16[2,2,96,768]{3,2,1,0:T(8,128)(2,1)}, bf16[2,2,96,768]{3,2,1,0:T(8,128)(2,1)}, u32[]{:S(2)}, u32[]{:S(2)}) collective-permute-start(bf16[2,2,96,768]{3,2,1,0:T(8,128)(2,1)} %get-tuple-element.379), channel_id=1, source_target_pairs={{0,15},{1,0},{2,1},{3,2},{4,3},{5,4},{6,5},{7,6},{8,7},{9,8},{10,9... | collective-permute-start | bytes 1769480 | tf_op jit(solution)/shard_map/ppermute | solution.py:11
  6.2 38.4 %collective-permute-start.12 = (bf16[2,2,96,768]{3,2,1,0:T(8,128)(2,1)}, bf16[2,2,96,768]{3,2,1,0:T(8,128)(2,1)}, u32[]{:S(2)}, u32[]{:S(2)}) collective-permute-start(bf16[2,2,96,768]{3,2,1,0:T(8,128)(2,1)} %get-tuple-element.378), channel_id=1, source_target_pairs={{0,240},{16,0},{32,16},{48,32},{64,48},{80,64},{96,80},{112,96},{1... | collective-permute-start | bytes 1769480 | tf_op jit(solution)/shard_map/ppermute | solution.py:11
  12.2 3.1 %copy-start.9 = (s32[2,3,2]{1,2,0:T(2,128)S(1)}, s32[2,3,2]{1,2,0:T(2,128)}, u32[]{:S(2)}) copy-start(s32[2,3,2]{1,2,0:T(2,128)} %param.61) | copy-start | bytes 148
  12.2 16.2 %copy-start = (bf16[1,1,2,2,2,96,768]{6,5,4,3,2,1,0:T(8,128)(2,1)S(1)}, bf16[1,1,2,2,2,96,768]{6,5,4,3,2,1,0:T(8,128)(2,1)}, u32[]{:S(2)}) copy-start(bf16[1,1,2,2,2,96,768]{6,5,4,3,2,1,0:T(8,128)(2,1)} %param.56) | copy-start | bytes 3538948
  12.3 27.6 %collective-permute-start.14 = (bf16[2,2,96,128]{3,2,1,0:T(8,128)(2,1)}, bf16[2,2,96,128]{3,2,1,0:T(8,128)(2,1)}, u32[]{:S(2)}, u32[]{:S(2)}) collective-permute-start(bf16[2,2,96,128]{3,2,1,0:T(8,128)(2,1)} %bitcast.96), channel_id=1, source_target_pairs={{0,240},{16,0},{32,16},{48,32},{64,48},{80,64},{96,80},{112,96},{1... | collective-permute-start | bytes 294920 | tf_op jit(solution)/shard_map/ppermute | solution.py:11
  14.3 49.4 %collective-permute-start.1 = (bf16[2,2,96,768]{3,2,1,0:T(8,128)(2,1)}, bf16[2,2,96,768]{3,2,1,0:T(8,128)(2,1)}, u32[]{:S(2)}, u32[]{:S(2)}) collective-permute-start(bf16[2,2,96,768]{3,2,1,0:T(8,128)(2,1)} %get-tuple-element.385), channel_id=1, source_target_pairs={{0,1},{1,2},{2,3},{3,4},{4,5},{5,6},{6,7},{7,8},{8,9},{9,10},{10,1... | collective-permute-start | bytes 1769480 | tf_op jit(solution)/shard_map/ppermute | solution.py:11
  14.3 25.5 %collective-permute-start.2 = (bf16[2,2,96,128]{3,2,1,0:T(8,128)(2,1)}, bf16[2,2,96,128]{3,2,1,0:T(8,128)(2,1)}, u32[]{:S(2)}, u32[]{:S(2)}) collective-permute-start(bf16[2,2,96,128]{3,2,1,0:T(8,128)(2,1)} %bitcast.16), channel_id=1, source_target_pairs={{0,16},{16,32},{32,48},{48,64},{64,80},{80,96},{96,112},{112,128},... | collective-permute-start | bytes 294920 | tf_op jit(solution)/shard_map/ppermute | solution.py:11
  30.2 5.9 %copy-start.10 = (s32[4]{0:T(128)S(1)}, s32[4]{0:T(128)}, u32[]{:S(2)}) copy-start(s32[4]{0:T(128)} %constant.560.clone.1) | copy-start | bytes 52
  39.9 25.2 %collective-permute-start = (bf16[2,2,96,768]{3,2,1,0:T(8,128)(2,1)}, bf16[2,2,96,768]{3,2,1,0:T(8,128)(2,1)S(1)}, u32[]{:S(2)}, u32[]{:S(2)}) collective-permute-start(bf16[2,2,96,768]{3,2,1,0:T(8,128)(2,1)} %get-tuple-element.384), channel_id=1, source_target_pairs={{0,16},{16,32},{32,48},{48,64},{64,80},{80,96},{96,112},{112,128},... | collective-permute-start | bytes 1769480 | tf_op jit(solution)/shard_map/ppermute | solution.py:11
  39.9 17.3 %collective-permute-start.15 = (bf16[2,2,96,128]{3,2,1,0:T(8,128)(2,1)}, bf16[2,2,96,128]{3,2,1,0:T(8,128)(2,1)S(1)}, u32[]{:S(2)}, u32[]{:S(2)}) collective-permute-start(bf16[2,2,96,128]{3,2,1,0:T(8,128)(2,1)} %collective-permute-done.14), channel_id=1, source_target_pairs={{0,15},{1,0},{2,1},{3,2},{4,3},{5,4},{6,5},{7,6},{8,7},{9,8},{10,9... | collective-permute-start | bytes 294920 | tf_op jit(solution)/shard_map/ppermute | solution.py:11
  43.5 58.1 %collective-permute-start.3 = (bf16[2,2,96,128]{3,2,1,0:T(8,128)(2,1)}, bf16[2,2,96,128]{3,2,1,0:T(8,128)(2,1)S(1)}, u32[]{:S(2)}, u32[]{:S(2)}) collective-permute-start(bf16[2,2,96,128]{3,2,1,0:T(8,128)(2,1)} %collective-permute-done.2), channel_id=1, source_target_pairs={{0,1},{1,2},{2,3},{3,4},{4,5},{5,6},{6,7},{7,8},{8,9},{9,10},{10,1... | collective-permute-start | bytes 294920 | tf_op jit(solution)/shard_map/ppermute | solution.py:11
  45.6 28.4 %slice-start = ((s8[4718592]{0:T(1024)(128)(4,1)}), s8[4194304]{0:T(1024)(128)(4,1)S(1)}, s32[]{:S(2)}) async-start(s8[4718592]{0:T(1024)(128)(4,1)} %bitcast.395), calls=%async_computation | async-start | bytes 8388608
  50.1 23.8 %slice-start.1 = ((s8[4718592]{0:T(1024)(128)(4,1)}), s8[524288]{0:T(1024)(128)(4,1)S(1)}, s32[]{:S(2)}) async-start(s8[4718592]{0:T(1024)(128)(4,1)} %bitcast.395), calls=%async_computation.1 | async-start | bytes 1048576
  58.1 4.2 %copy-start.6 = (bf16[2,2,96,128]{3,2,1,0:T(8,128)(2,1)S(1)}, bf16[2,2,96,128]{3,2,1,0:T(8,128)(2,1)}, u32[]{:S(2)}) copy-start(bf16[2,2,96,128]{3,2,1,0:T(8,128)(2,1)} %copy.38) | copy-start | bytes 294916
  58.2 15.6 %collective-permute-start.16 = (bf16[2,2,96,768]{3,2,1,0:T(8,128)(2,1)S(1)}, bf16[2,2,96,768]{3,2,1,0:T(8,128)(2,1)S(1)}, u32[]{:S(2)}, u32[]{:S(2)}) collective-permute-start(bf16[2,2,96,768]{3,2,1,0:T(8,128)(2,1)S(1)} %get-tuple-element.376), channel_id=1, source_target_pairs={{0,240},{16,0},{32,16},{48,32},{64,48},{80,64},{96,80},{112,96},{1... | collective-permute-start | bytes 1769480 | tf_op jit(solution)/shard_map/ppermute | solution.py:11
  58.3 15.6 %collective-permute-start.17 = (bf16[2,2,96,768]{3,2,1,0:T(8,128)(2,1)S(1)}, bf16[2,2,96,768]{3,2,1,0:T(8,128)(2,1)S(1)}, u32[]{:S(2)}, u32[]{:S(2)}) collective-permute-start(bf16[2,2,96,768]{3,2,1,0:T(8,128)(2,1)S(1)} %get-tuple-element.377), channel_id=1, source_target_pairs={{0,15},{1,0},{2,1},{3,2},{4,3},{5,4},{6,5},{7,6},{8,7},{9,8},{10,9... | collective-permute-start | bytes 1769480 | tf_op jit(solution)/shard_map/ppermute | solution.py:11
  63.8 6.5 %collective-permute-start.18 = (bf16[2,2,96,128]{3,2,1,0:T(8,128)(2,1)S(1)}, bf16[2,2,96,128]{3,2,1,0:T(8,128)(2,1)S(1)}, u32[]{:S(2)}, u32[]{:S(2)}) collective-permute-start(bf16[2,2,96,128]{3,2,1,0:T(8,128)(2,1)S(1)} %fusion.104), channel_id=1, source_target_pairs={{0,240},{16,0},{32,16},{48,32},{64,48},{80,64},{96,80},{112,96},{1... | collective-permute-start | bytes 294920 | tf_op jit(solution)/shard_map/ppermute | solution.py:11
  70.3 6.3 %collective-permute-start.19 = (bf16[2,2,96,128]{3,2,1,0:T(8,128)(2,1)S(1)}, bf16[2,2,96,128]{3,2,1,0:T(8,128)(2,1)S(1)}, u32[]{:S(2)}, u32[]{:S(2)}) collective-permute-start(bf16[2,2,96,128]{3,2,1,0:T(8,128)(2,1)S(1)} %collective-permute-done.18), channel_id=1, source_target_pairs={{0,15},{1,0},{2,1},{3,2},{4,3},{5,4},{6,5},{7,6},{8,7},{9,8},{10,9... | collective-permute-start | bytes 294920 | tf_op jit(solution)/shard_map/ppermute | solution.py:11
  77.6 20.8 %collective-permute-start.20 = (bf16[2,2,96,768]{3,2,1,0:T(8,128)(2,1)S(1)}, bf16[2,2,96,768]{3,2,1,0:T(8,128)(2,1)S(1)}, u32[]{:S(2)}, u32[]{:S(2)}) collective-permute-start(bf16[2,2,96,768]{3,2,1,0:T(8,128)(2,1)S(1)} %get-tuple-element.374), channel_id=1, source_target_pairs={{0,240},{16,0},{32,16},{48,32},{64,48},{80,64},{96,80},{112,96},{1... | collective-permute-start | bytes 1769480 | tf_op jit(solution)/shard_map/ppermute | solution.py:11
  86.9 11.8 %collective-permute-start.21 = (bf16[2,2,96,768]{3,2,1,0:T(8,128)(2,1)S(1)}, bf16[2,2,96,768]{3,2,1,0:T(8,128)(2,1)S(1)}, u32[]{:S(2)}, u32[]{:S(2)}) collective-permute-start(bf16[2,2,96,768]{3,2,1,0:T(8,128)(2,1)S(1)} %get-tuple-element.375), channel_id=1, source_target_pairs={{0,15},{1,0},{2,1},{3,2},{4,3},{5,4},{6,5},{7,6},{8,7},{9,8},{10,9... | collective-permute-start | bytes 1769480 | tf_op jit(solution)/shard_map/ppermute | solution.py:11
  91.9 4.7 %collective-permute-start.22 = (bf16[2,2,96,128]{3,2,1,0:T(8,128)(2,1)S(1)}, bf16[2,2,96,128]{3,2,1,0:T(8,128)(2,1)S(1)}, u32[]{:S(2)}, u32[]{:S(2)}) collective-permute-start(bf16[2,2,96,128]{3,2,1,0:T(8,128)(2,1)S(1)} %fusion.107), channel_id=1, source_target_pairs={{0,240},{16,0},{32,16},{48,32},{64,48},{80,64},{96,80},{112,96},{1... | collective-permute-start | bytes 294920 | tf_op jit(solution)/shard_map/ppermute | solution.py:11
  96.6 9.8 %collective-permute-start.23 = (bf16[2,2,96,128]{3,2,1,0:T(8,128)(2,1)S(1)}, bf16[2,2,96,128]{3,2,1,0:T(8,128)(2,1)S(1)}, u32[]{:S(2)}, u32[]{:S(2)}) collective-permute-start(bf16[2,2,96,128]{3,2,1,0:T(8,128)(2,1)S(1)} %collective-permute-done.22), channel_id=1, source_target_pairs={{0,15},{1,0},{2,1},{3,2},{4,3},{5,4},{6,5},{7,6},{8,7},{9,8},{10,9... | collective-permute-start | bytes 294920 | tf_op jit(solution)/shard_map/ppermute | solution.py:11
  103.8 19.6 %collective-permute-start.4 = (bf16[2,2,96,768]{3,2,1,0:T(8,128)(2,1)S(1)}, bf16[2,2,96,768]{3,2,1,0:T(8,128)(2,1)S(1)}, u32[]{:S(2)}, u32[]{:S(2)}) collective-permute-start(bf16[2,2,96,768]{3,2,1,0:T(8,128)(2,1)S(1)} %get-tuple-element.382), channel_id=1, source_target_pairs={{0,16},{16,32},{32,48},{48,64},{64,80},{80,96},{96,112},{112,128},... | collective-permute-start | bytes 1769480 | tf_op jit(solution)/shard_map/ppermute | solution.py:11
  106.0 17.4 %collective-permute-start.6 = (bf16[2,2,96,128]{3,2,1,0:T(8,128)(2,1)S(1)}, bf16[2,2,96,128]{3,2,1,0:T(8,128)(2,1)S(1)}, u32[]{:S(2)}, u32[]{:S(2)}) collective-permute-start(bf16[2,2,96,128]{3,2,1,0:T(8,128)(2,1)S(1)} %fusion.98), channel_id=1, source_target_pairs={{0,16},{16,32},{32,48},{48,64},{64,80},{80,96},{96,112},{112,128},... | collective-permute-start | bytes 294920 | tf_op jit(solution)/shard_map/ppermute | solution.py:11
  106.3 24.9 %collective-permute-start.5 = (bf16[2,2,96,768]{3,2,1,0:T(8,128)(2,1)S(1)}, bf16[2,2,96,768]{3,2,1,0:T(8,128)(2,1)S(1)}, u32[]{:S(2)}, u32[]{:S(2)}) collective-permute-start(bf16[2,2,96,768]{3,2,1,0:T(8,128)(2,1)S(1)} %get-tuple-element.383), channel_id=1, source_target_pairs={{0,1},{1,2},{2,3},{3,4},{4,5},{5,6},{6,7},{7,8},{8,9},{9,10},{10,1... | collective-permute-start | bytes 1769480 | tf_op jit(solution)/shard_map/ppermute | solution.py:11
  123.4 10.4 %collective-permute-start.7 = (bf16[2,2,96,128]{3,2,1,0:T(8,128)(2,1)S(1)}, bf16[2,2,96,128]{3,2,1,0:T(8,128)(2,1)S(1)}, u32[]{:S(2)}, u32[]{:S(2)}) collective-permute-start(bf16[2,2,96,128]{3,2,1,0:T(8,128)(2,1)S(1)} %collective-permute-done.6), channel_id=1, source_target_pairs={{0,1},{1,2},{2,3},{3,4},{4,5},{5,6},{6,7},{7,8},{8,9},{9,10},{10,1... | collective-permute-start | bytes 294920 | tf_op jit(solution)/shard_map/ppermute | solution.py:11
  134.8 26.0 %collective-permute-start.9 = (bf16[2,2,96,768]{3,2,1,0:T(8,128)(2,1)S(1)}, bf16[2,2,96,768]{3,2,1,0:T(8,128)(2,1)S(1)}, u32[]{:S(2)}, u32[]{:S(2)}) collective-permute-start(bf16[2,2,96,768]{3,2,1,0:T(8,128)(2,1)S(1)} %get-tuple-element.381), channel_id=1, source_target_pairs={{0,1},{1,2},{2,3},{3,4},{4,5},{5,6},{6,7},{7,8},{8,9},{9,10},{10,1... | collective-permute-start | bytes 1769480 | tf_op jit(solution)/shard_map/ppermute | solution.py:11
  134.9 25.9 %collective-permute-start.8 = (bf16[2,2,96,768]{3,2,1,0:T(8,128)(2,1)S(1)}, bf16[2,2,96,768]{3,2,1,0:T(8,128)(2,1)S(1)}, u32[]{:S(2)}, u32[]{:S(2)}) collective-permute-start(bf16[2,2,96,768]{3,2,1,0:T(8,128)(2,1)S(1)} %get-tuple-element.380), channel_id=1, source_target_pairs={{0,16},{16,32},{32,48},{48,64},{64,80},{80,96},{96,112},{112,128},... | collective-permute-start | bytes 1769480 | tf_op jit(solution)/shard_map/ppermute | solution.py:11
  135.7 2.6 %copy-start.7 = (bf16[1,1,2,2,96,128]{5,4,3,2,1,0:T(8,128)(2,1)}, bf16[1,1,2,2,96,128]{5,4,3,2,1,0:T(8,128)(2,1)S(1)}, u32[]{:S(2)}) copy-start(bf16[1,1,2,2,96,128]{5,4,3,2,1,0:T(8,128)(2,1)S(1)} %fusion.115) | copy-start | bytes 294916
  136.4 13.2 %collective-permute-start.10 = (bf16[2,2,96,128]{3,2,1,0:T(8,128)(2,1)S(1)}, bf16[2,2,96,128]{3,2,1,0:T(8,128)(2,1)S(1)}, u32[]{:S(2)}, u32[]{:S(2)}) collective-permute-start(bf16[2,2,96,128]{3,2,1,0:T(8,128)(2,1)S(1)} %fusion.101), channel_id=1, source_target_pairs={{0,16},{16,32},{32,48},{48,64},{64,80},{80,96},{96,112},{112,128},... | collective-permute-start | bytes 294920 | tf_op jit(solution)/shard_map/ppermute | solution.py:11
  149.6 13.9 %collective-permute-start.11 = (bf16[2,2,96,128]{3,2,1,0:T(8,128)(2,1)S(1)}, bf16[2,2,96,128]{3,2,1,0:T(8,128)(2,1)S(1)}, u32[]{:S(2)}, u32[]{:S(2)}) collective-permute-start(bf16[2,2,96,128]{3,2,1,0:T(8,128)(2,1)S(1)} %collective-permute-done.10), channel_id=1, source_target_pairs={{0,1},{1,2},{2,3},{3,4},{4,5},{5,6},{6,7},{7,8},{8,9},{9,10},{10,1... | collective-permute-start | bytes 294920 | tf_op jit(solution)/shard_map/ppermute | solution.py:11
  (5 other events, 5.6 us)
where the time goes:
time: 167 us
  waiting for transfers between devices  62.4 us (37%)
  starting transfers between devices  37 us (22%)
  other arithmetic  22.4 us (13%)
  local copies, waits for them, and re-layouts  18 us (11%)
  matrix products  14.5 us (9%)
  between operations  12.3 us (7%)
    ppermute x24, waiting for transfers between devices, from_behind(): lax.ppermute(array, axis, [(i, (i + by) % count) for i in range(count)])  62.4 us
    ppermute x24, starting transfers between devices, from_behind(): lax.ppermute(array, axis, [(i, (i + by) % count) for i in range(count)])  37 us
    dot_general x6, matrix products, trace_update(): jnp.einsum(form, stacked, cell_operators, preferred_element_type=jnp.floa...  14.5 us
    unnamed x36, local copies, waits for them, and re-layouts  8.88 us
    scatter x6, other arithmetic, sweep_tick(): corner_states = corner_states.at[chosen].set(new_corner)  5.46 us
    scatter x6, other arithmetic, sweep_tick(): states = states.at[:, chosen].set(jnp.stack([new_first, new_second]))  4.74 us
    another operation x6, other arithmetic, sweep_tick(): chosen = jnp.argmax((front_plan == klass).astype(jnp.int32))  4.04 us
    squeeze x6, local copies, waits for them, and re-layouts, sweep_tick(): first_send = states[0]  3.82 us
  transfers between devices with their start and end apart: 24, of which 8 were waited for; matrix products, arithmetic and copies ran while one was open for 28% of the time, Pallas kernels for 0%

commit v1 on v0

v1 whole, which is shorter than its diff:
```python
import jax
import jax.numpy as jnp
from jax import lax
from jax.experimental import pallas as pl
from jax.experimental.pallas import tpu as pltpu
from jax.sharding import PartitionSpec as P

MESH = pl.DeviceIdType.MESH
TICKS = 3
CHUNKS = 2


def sweep_kernel(
    sizes,
    roster,
    se_edges,
    nw_edges,
    se_corners,
    nw_corners,
    operators,
    sources,
    se_out,
    nw_out,
    se_corner_out,
    nw_corner_out,
    held_se,
    held_nw,
    weights,
    flipped,
    source,
    sent,
    got,
    start_se,
    start_nw,
    corner_got,
    corner_now,
    corner_new,
    plan,
    load_sem,
    send_sem,
    recv_sem,
    corner_send_sem,
    corner_recv_sem,
):
    row_count, col_count, shots, width, corner = sizes
    part = shots // CHUNKS
    row = lax.axis_index("row")
    col = lax.axis_index("col")
    down = lax.rem(row + 1, row_count)
    up = lax.rem(row + row_count - 1, row_count)
    right = lax.rem(col + 1, col_count)
    left = lax.rem(col + col_count - 1, col_count)
    ahead = (
        ((down, col), (row, right), (down, right)),
        ((up, col), (row, left), (up, left)),
    )

    loads = [
        pltpu.make_async_copy(se_edges, held_se, load_sem.at[0]),
        pltpu.make_async_copy(nw_edges, held_nw, load_sem.at[1]),
        pltpu.make_async_copy(operators, weights, load_sem.at[2]),
        pltpu.make_async_copy(sources, source, load_sem.at[3]),
        pltpu.make_async_copy(roster, plan, load_sem.at[4]),
    ]
    for load in loads:
        load.start()

    barrier = pltpu.get_barrier_semaphore()
    for direction in ahead:
        for place in direction:
            pl.semaphore_signal(barrier, inc=1, device_id=place, device_id_type=MESH)

    loads[4].wait()
    klass = lax.rem(row + col, 2)
    first = [jnp.where(plan[d, 0, 0] == klass, 0, 1) for d in range(2)]

    def edge_copy(k, d, slot, chunk):
        return pltpu.make_async_remote_copy(
            src_ref=sent.at[k, d, slot, chunk],
            dst_ref=got.at[k, d, slot, chunk],
            send_sem=send_sem.at[k, d, slot, chunk],
            recv_sem=recv_sem.at[k, d, slot, chunk],
            device_id=ahead[d][slot],
            device_id_type=MESH,
        )

    def corner_start_copy(d):
        return pltpu.make_async_remote_copy(
            src_ref=(se_corners, nw_corners)[d],
            dst_ref=(start_se, start_nw)[d],
            send_sem=corner_send_sem.at[0, d],
            recv_sem=corner_recv_sem.at[0, d],
            device_id=ahead[d][2],
            device_id_type=MESH,
        )

    def corner_copy(d):
        return pltpu.make_async_remote_copy(
            src_ref=corner_new.at[d],
            dst_ref=corner_got.at[d],
            send_sem=corner_send_sem.at[1, d],
            recv_sem=corner_recv_sem.at[1, d],
            device_id=ahead[d][2],
            device_id_type=MESH,
        )

    for d in range(2):
        loads[d].wait()
        for chunk in range(CHUNKS):
            for slot in range(2):
                sent[0, d, slot, chunk] = (held_se, held_nw)[d][slot, 1 - first[d], :, chunk * part : (chunk + 1) * part, :]
    pl.semaphore_wait(barrier, 6)
    for chunk in range(CHUNKS):
        for d in range(2):
            for slot in range(2):
                edge_copy(0, d, slot, chunk).start()
    for d in range(2):
        corner_start_copy(d).start()

    loads[2].wait()
    for m in range(4):
        flipped[m] = weights[m].T
    loads[3].wait()
    def update(k, d, chunk):
        rows = slice(chunk * part, (chunk + 1) * part)
        batch = lax.rem(first[d] + k, 2)
        for slot in range(2):
            edge_copy(k, d, slot, chunk).wait_recv()
        a_re, a_im = got[k, d, 0, chunk, 0], got[k, d, 0, chunk, 1]
        b_re, b_im = got[k, d, 1, chunk, 0], got[k, d, 1, chunk, 1]
        table = (weights, flipped)[d]
        stacks = (
            (a_re, a_im, b_re, b_im),
            (-a_im, a_re, -b_im, b_re),
            (b_re, b_im, a_re, a_im),
            (-b_im, b_re, -a_im, a_re),
        )
        total = None
        for m, stack in enumerate(stacks):
            term = jnp.dot(jnp.concatenate(stack, 0), table[m], preferred_element_type=jnp.float32)
            total = term if total is None else total + term
        total = total.reshape(2, 2, part, width)
        near, far = slice(0, corner), slice(width - corner, width)
        if d == 1:
            near, far = far, near
        for plane in range(2):
            extra = source[batch, plane, rows, :].astype(jnp.float32)
            cornered = corner_now[d, plane, rows, :].astype(jnp.float32)
            both = []
            for slot in range(2):
                value = total[slot, plane] + extra
                if d == 0:
                    value = jnp.concatenate([value[:, near] + cornered, value[:, corner:]], 1)
                else:
                    value = jnp.concatenate([value[:, : width - corner], value[:, near] + cornered], 1)
                both.append(value[:, far])
                value = value.astype(jnp.bfloat16)

                @pl.when(k < 2)
                def _():
                    sent[k + 1, d, slot, chunk, plane] = value

                @pl.when(k >= 1)
                def _():
                    (se_out, nw_out)[d][2 - k, slot, chunk, plane] = value

            value = (0.5 * (both[0] + both[1])).astype(jnp.bfloat16)

            @pl.when(k == 0)
            def _():
                corner_new[d, plane, rows, :] = value

            @pl.when(k >= 1)
            def _():
                (se_corner_out, nw_corner_out)[d][2 - k, plane, rows, :] = value


    def tick(k, carry):
        for d in range(2):

            @pl.when(k == 0)
            def _():
                corner_start_copy(d).wait_recv()

            @pl.when(k < 2)
            def _():
                corner_now[d] = (start_se, start_nw)[d][lax.rem(first[d] + k, 2)]

            @pl.when(k == 2)
            def _():
                corner_copy(d).wait_recv()
                corner_now[d] = corner_got[d]

        for chunk in range(CHUNKS):
            for d in range(2):
                update(k, d, chunk)

                @pl.when(k < 2)
                def _():
                    for slot in range(2):
                        edge_copy(k + 1, d, slot, chunk).start()

                if chunk == CHUNKS - 1:

                    @pl.when(k == 0)
                    def _():
                        corner_copy(d).start()

        return carry

    lax.fori_loop(0, TICKS, tick, 0)

    for d in range(2):
        corner_start_copy(d).wait_send()
        corner_copy(d).wait_send()
        for slot in range(2):
            for chunk in range(CHUNKS):
                for k in range(TICKS):
                    edge_copy(k, d, slot, chunk).wait_send()


def place_kernel(roster, se, nw, se_corner, nw_corner, se_out, nw_out, se_corner_out, nw_corner_out, plan, sem, plan_sem):
    load = pltpu.make_async_copy(roster, plan, plan_sem)
    load.start()
    load.wait()
    klass = lax.rem(lax.axis_index("row") + lax.axis_index("col"), 2)
    part = se.shape[4]
    copies = []
    for d in range(2):
        first = jnp.where(plan[d, 0, 0] == klass, 0, 1)
        for late in range(2):
            batch = first if late == 0 else 1 - first
            copies.append(((se_corner, nw_corner)[d].at[late], (se_corner_out, nw_corner_out)[d].at[batch]))
            for slot in range(2):
                for chunk in range(CHUNKS):
                    copies.append(
                        (
                            (se, nw)[d].at[late, slot, chunk],
                            (se_out, nw_out)[d].at[slot, batch, :, pl.ds(chunk * part, part), :],
                        )
                    )
    copies = [pltpu.make_async_copy(a, b, sem.at[i]) for i, (a, b) in enumerate(copies)]
    for copy in copies:
        copy.start()
    for copy in copies:
        copy.wait()


def shards(
    southeast_edges,
    northwest_edges,
    southeast_corners,
    northwest_corners,
    operators,
    sources,
    roster,
):
    row_count, col_count = lax.axis_size("row"), lax.axis_size("col")
    shots, width = sources.shape[-2:]
    corner = southeast_corners.shape[-1]
    part = shots // CHUNKS
    sizes = (row_count, col_count, shots, width, corner)
    anywhere = pl.BlockSpec(memory_space=pltpu.HBM)
    inside = pl.BlockSpec(memory_space=pltpu.VMEM)
    part_shape = jax.ShapeDtypeStruct((2, 2, CHUNKS, 2, part, width), jnp.bfloat16)
    edge_shape = jax.ShapeDtypeStruct((2, 2, 2, shots, width), jnp.bfloat16)
    corner_shape = jax.ShapeDtypeStruct((2, 2, shots, corner), jnp.bfloat16)
    bf16 = jnp.bfloat16
    plan = jnp.swapaxes(roster, 1, 2)
    results = pl.pallas_call(
        lambda *refs: sweep_kernel(sizes, *refs),
        out_shape=tuple(
            pltpu.VMEM(shape.shape, shape.dtype)
            for shape in (part_shape, part_shape, corner_shape, corner_shape)
        ),
        in_specs=[anywhere] * 7,
        out_specs=(inside,) * 4,
        scratch_shapes=[
            pltpu.VMEM((2, 2, 2, shots, width), bf16),
            pltpu.VMEM((2, 2, 2, shots, width), bf16),
            pltpu.VMEM((4, width, width), bf16),
            pltpu.VMEM((4, width, width), bf16),
            pltpu.VMEM((2, 2, shots, width), bf16),
            pltpu.VMEM((TICKS, 2, 2, CHUNKS, 2, part, width), bf16),
            pltpu.VMEM((TICKS, 2, 2, CHUNKS, 2, part, width), bf16),
            pltpu.VMEM((2, 2, shots, corner), bf16),
            pltpu.VMEM((2, 2, shots, corner), bf16),
            pltpu.VMEM((2, 2, shots, corner), bf16),
            pltpu.VMEM((2, 2, shots, corner), bf16),
            pltpu.VMEM((2, 2, shots, corner), bf16),
            pltpu.SMEM((2, 2, TICKS), jnp.int32),
            pltpu.SemaphoreType.DMA((5,)),
            pltpu.SemaphoreType.DMA((TICKS, 2, 2, CHUNKS)),
            pltpu.SemaphoreType.DMA((TICKS, 2, 2, CHUNKS)),
            pltpu.SemaphoreType.DMA((2, 2)),
            pltpu.SemaphoreType.DMA((2, 2)),
        ],
        compiler_params=pltpu.CompilerParams(
            collective_id=0, has_side_effects=True, vmem_limit_bytes=40 << 20
        ),
        name="sweep",
    )(
        *(
            pltpu.with_memory_space_constraint(array, pltpu.HBM)
            for array in (
                plan,
                southeast_edges[0, 0],
                northwest_edges[0, 0],
                southeast_corners[0, 0],
                northwest_corners[0, 0],
                operators[0, 0].reshape(4, width, width),
                sources[0, 0],
            )
        )
    )
    outs = pl.pallas_call(
        place_kernel,
        out_shape=(edge_shape, edge_shape, corner_shape, corner_shape),
        in_specs=[anywhere] + [inside] * 4,
        out_specs=(anywhere,) * 4,
        scratch_shapes=[
            pltpu.SMEM((2, 2, TICKS), jnp.int32),
            pltpu.SemaphoreType.DMA((4 + 8 * CHUNKS,)),
            pltpu.SemaphoreType.DMA,
        ],
        compiler_params=pltpu.CompilerParams(vmem_limit_bytes=8 << 20),
        name="place",
    )(plan, *results)
    return tuple(out[None, None] for out in outs)


def solution(mesh):
    edges = P("row", "col", None, None, None, None, None)
    corners = P("row", "col", None, None, None, None)
    return jax.shard_map(
        shards,
        mesh=mesh,
        in_specs=(edges, edges, corners, corners, corners, corners, P()),
        out_specs=(edges, edges, corners, corners),
        check_vma=False,
    )
```

time: 167 us -> 56.8 us (0.34)
  the two profiles are of different devices: /device:TPU:4 before, /device:TPU:27 now
where the time goes in v1:
time: 56.8 us
  Pallas kernels  56.1 us (99%)
  between operations  0.66 us (1%)
    pallas_call x1, Pallas kernels, shards(): pl.pallas_call(lambda *refs: sweep_kernel(sizes, *refs), out_shape=tuple(...  53.9 us
    pallas_call x1, Pallas kernels, shards(): pl.pallas_call(place_kernel, out_shape=(edge_shape, edge_shape, corner_sh...  2.22 us

profile of v1, /device:TPU:27, one launch (start us, length us, event | category | flops | bytes accessed | tf_op | source)
XLA Modules:
  0.0 56.8 jit_solution(2120662862899320215)
XLA Ops:
  0.6 0.0 copy-start
  0.6 53.9 %sweep.1 = (bf16[2,2,2,2,48,768]{5,4,3,2,1,0:T(8,128)(2,1)S(1)}, bf16[2,2,2,2,48,768]{5,4,3,2,1,0:T(8,128)(2,1)S(1)}, bf16[2,2,96,128]{3,2,1,0:T(8,128)(2,1)S(1)}, bf16[2,2,96,128]{3,2,1,0:T(8,128)(2,1)S(1)}) custom-call(s32[2,2,3]{2,1,0:T(2,128)} %bitcast.11, bf16[2,2,2,96,768]{4,3,2,1,0:T(8,128)(2,1)} %bitcast.14, bf16[2,2,2,96,768]{4,3,2,1,0:T(8,128)(2,1)} %bitcast.15, ...), custom_call_target="tpu_custom_call" | custom-call | tf_op jit(solution)/shard_map/sweep/pallas_call | solution.py:270
  54.5 0.0 copy-done
  54.5 2.2 %place.1 = (bf16[2,2,2,96,768]{4,3,2,1,0:T(8,128)(2,1)}, bf16[2,2,2,96,768]{4,3,2,1,0:T(8,128)(2,1)}, bf16[2,2,96,128]{3,2,1,0:T(8,128)(2,1)}, bf16[2,2,96,128]{3,2,1,0:T(8,128)(2,1)}) custom-call(s32[2,2,3]{2,1,0:T(2,128)S(1)} %bitcast.12, bf16[2,2,2,2,48,768]{5,4,3,2,1,0:T(8,128)(2,1)S(1)} %get-tuple-element.12.se, ...), custom_call_target="tpu_custom_call" | custom-call | tf_op jit(solution)/shard_map/place/pallas_call | solution.py:316
Async XLA Ops:
  0.6 53.9 %copy-start = (s32[2,3,2]{1,2,0:T(2,128)S(1)}, s32[2,3,2]{1,2,0:T(2,128)}, u32[]{:S(2)}) copy-start(s32[2,3,2]{1,2,0:T(2,128)} %param.13) | copy-start | bytes 148
